TPU v7x, 256 devices: a whole 4x4x8 slice. The times are simulated.
256 devices in a mesh: blk: 64 (over x, y_hi, z), rep: 4 (over y_lo, core).
Axes of the slice: x: 4, y: 4 (y_hi: 2, y_lo: 2; y = y_hi * 2 + y_lo), z: 8, core: 2. Of those that a mesh axis runs over, the one named last changes fastest.
Arguments:
- embeddings: float32 [131072, 768], P(('blk', 'rep')), may hold values from -6 to 6
- ranks: int32 [131072], replicated, may hold values from 0 to 131071, each once
Outputs:
- earlier_best: float32 [131072], P(('blk', 'rep'))
- later_best: float32 [131072], P(('blk', 'rep'))
Inputs may be any that keep to these rules, and one draw needn't show every extreme that they name: ranks is a permutation of 0 .. 131071.
All inputs are finite; a program needn't handle non-finite values.
Results may differ from a plain program's by a relative error of at most 0.0012.
Values may be sent and summed in bfloat16 or wider, within the bound.
A program may use at most 64 MiB of HBM per device.

v0:
```python
import jax
import jax.numpy as jnp
from jax import lax
from jax.sharding import PartitionSpec as P

STEPS = 3


def shifted(value, axis, steps):
    count = lax.axis_size(axis)
    pairs = [(source, (source + steps) % count) for source in range(count)]
    return lax.ppermute(value, axis, pairs)


def from_everyone(value, axis):
    peers = lax.axis_size(axis)
    return lax.all_to_all(
        jnp.broadcast_to(value[None], (peers, *value.shape)), axis, 0, 0, tiled=True
    )


def over_copies(value, axis):
    everything = from_everyone(value, axis)
    return jnp.max(everything, axis=0)


def best_pair(host, host_rank, visit, visit_rank):
    scores = lax.dot_general(
        host, visit, (((1,), (1,)), ((), ())), preferred_element_type=jnp.float32
    )
    kept = jnp.where(visit_rank[None, :] < host_rank[:, None], scores, jnp.float32(-1.0))
    return (jnp.max(kept, axis=1), jnp.max(kept, axis=0))


def shards(embeddings, ranks):
    rows = embeddings.shape[0]
    copies = lax.axis_size("rep")
    blocks = lax.axis_size("blk")
    span = rows * copies
    block_id = lax.axis_index("blk")
    copy_id = lax.axis_index("rep")
    squares = jnp.sum(embeddings * embeddings, axis=1, keepdims=True)
    unit = (embeddings * lax.rsqrt(squares + 1e-06)).astype(jnp.bfloat16)
    mine = copy_id * rows
    host = lax.all_gather(unit, "rep", axis=0, tiled=True)
    host_ranks = lax.dynamic_slice_in_dim(ranks, block_id * span, span)
    row_best = jnp.full((host.shape[0],), -1.0, jnp.float32)
    partials = []
    visit = unit
    part = unit
    for offset in range(STEPS + 1):
        if offset > 0:
            part = shifted(part, "blk", 1)
        visit = part
        start = (block_id - offset) % blocks * span + mine
        visit_rank = lax.dynamic_slice_in_dim(ranks, start, rows)
        row_part, column_part = best_pair(host, host_ranks, visit, visit_rank)
        row_best = jnp.maximum(row_best, row_part)
        partials.append(column_part)
    home = partials[0]
    for offset in range(1, STEPS + 1):
        home = jnp.maximum(home, shifted(partials[offset], "blk", -offset))
    row_merged = over_copies(row_best, "rep")
    return (lax.dynamic_slice_in_dim(row_merged, mine, rows), home)


def solution(mesh):
    return jax.shard_map(
        shards,
        mesh=mesh,
        in_specs=(P(("blk", "rep"), None), P()),
        out_specs=(P(("blk", "rep")), P(("blk", "rep"))),
        check_vma=False,
    )
```

profile of v0, /device:TPU:1, one launch (start us, length us, event | category | flops | bytes accessed | tf_op | source)
XLA Modules:
  0.0 122.9 jit_solution(6373545377933322261)
XLA Ops:
  7.2 0.0 copy-start.1
  7.2 0.0 all-gather.2.cloned.1.call-start
  7.2 1.6 %multiply_reduce_fusion = f32[512]{0:T(512)S(1)} fusion(f32[512,768]{1,0:T(8,128)} %param.2), kind=kLoop, calls=%fused_computation.13 | loop fusion | flops 785920 | bytes 1574912 | tf_op jit(solution)/shard_map/reduce_sum | solution.py:42
  8.9 2.4 %multiply_convert_fusion = bf16[512,768]{1,0:T(8,128)(2,1)} fusion(f32[512,768]{1,0:T(8,128)} %param.2, f32[512]{0:T(512)S(1)} %add_rsqrt_fusion), kind=kLoop, calls=%fused_computation.12 | loop fusion | flops 786432 | bytes 2361344 | tf_op jit(solution)/shard_map/convert_element_type | solution.py:43
  11.3 0.0 all-gather.2.cloned.1.call-update
  11.3 2.5 %collective-permute-start = (bf16[512,768]{1,0:T(8,128)(2,1)}, bf16[512,768]{1,0:T(8,128)(2,1)S(1)}, u32[]{:S(2)}, u32[]{:S(2)}) collective-permute-start(bf16[512,768]{1,0:T(8,128)(2,1)} %multiply_convert_fusion), channel_id=1, source_target_pairs={{0,4},{4,8},{8,12},{12,16},{16,20},{20,24},{24,28},{28,32},{32,36}... | collective-permute-start | bytes 2359304 | tf_op jit(solution)/shard_map/ppermute | solution.py:12
  13.9 26.2 %collective-permute-done = bf16[512,768]{1,0:T(8,128)(2,1)S(1)} collective-permute-done((bf16[512,768]{1,0:T(8,128)(2,1)}, bf16[512,768]{1,0:T(8,128)(2,1)S(1)}, u32[]{:S(2)}, u32[]{:S(2)}) %collective-permute-start) | collective-permute-done | bytes 786464 | tf_op jit(solution)/shard_map/ppermute | solution.py:12
  40.1 0.0 collective-permute-start.1
  40.1 0.0 copy-done.1
  40.1 0.1 fusion.8
  40.2 23.4 %collective-permute-done.1 = bf16[512,768]{1,0:T(8,128)(2,1)S(1)} collective-permute-done((bf16[512,768]{1,0:T(8,128)(2,1)S(1)}, bf16[512,768]{1,0:T(8,128)(2,1)S(1)}, u32[]{:S(2)}, u32[]{:S(2)}) %collective-permute-start.1) | collective-permute-done | bytes 786464 | tf_op jit(solution)/shard_map/ppermute | solution.py:12
  63.6 0.0 collective-permute-start.2
  63.6 32.7 %all-gather.2.cloned.1.call-done = bf16[2048,768]{1,0:T(8,128)(2,1)} async-done(((bf16[512,768]{1,0:T(8,128)(2,1)}), bf16[2048,768]{1,0:T(8,128)(2,1)}) %all-gather.2.cloned.1.call-update) | async-done | bytes 3145744 | tf_op jit(solution)/shard_map/all_gather | solution.py:45
  96.3 3.9 %fusion.11 = f32[2048,512]{1,0:T(8,128)S(1)} fusion(bf16[2048,768]{1,0:T(8,128)(2,1)} %all-gather.2.cloned.1.call-done, bf16[512,768]{1,0:T(8,128)(2,1)S(1)} %collective-permute-done.1), kind=kOutput, calls=%fused_computation.20 | convolution fusion | flops 1610612736 | bytes 8126464 | tf_op jit(solution)/shard_map/dot_general | solution.py:28
  100.2 0.0 copy-done.2
  100.2 1.8 %fusion.10 = f32[2048,512]{1,0:T(8,128)S(1)} fusion(bf16[2048,768]{1,0:T(8,128)(2,1)S(1)} %copy-done.2, bf16[512,768]{1,0:T(8,128)(2,1)S(1)} %collective-permute-done), kind=kOutput, calls=%fused_computation.19 | convolution fusion | flops 1610612736 | bytes 8126464 | tf_op jit(solution)/shard_map/dot_general | solution.py:28
  102.0 0.0 dynamic-slice-start
  102.0 1.8 %fusion.9 = f32[2048,512]{1,0:T(8,128)S(1)} fusion(bf16[2048,768]{1,0:T(8,128)(2,1)S(1)} %copy-done.2, bf16[512,768]{1,0:T(8,128)(2,1)S(1)} %copy-done), kind=kOutput, calls=%fused_computation.18 | convolution fusion | flops 1610612736 | bytes 8126464 | tf_op jit(solution)/shard_map/dot_general | solution.py:28
  103.9 0.0 collective-permute-done.2
  103.9 0.0 dynamic-slice-done
  103.9 3.7 %fusion.2 = (f32[512]{0:T(512)S(1)}, f32[2048]{0:T(1024)S(1)}, f32[2048]{0:T(1024)S(1)}, f32[512]{0:T(512)S(1)}, f32[2048]{0:T(1024)S(1)}, /*index=5*/f32[512]{0:T(512)S(1)}, f32[2048]{0:T(1024)S(1)}, f32[512]{0:T(512)S(1)}) fusion(f32[2048,512]{1,0:T(8,128)S(1)} %fusion.10, s32[512]{0:T(512)S(1)} %get-tuple-element.17, s32[2048]{0:T(1024)S(1)} %dynamic-slice-done, ...), kind=kOutput, calls=%fused_computation.6 | convolution fusion | flops 1627379712 | bytes 16572416 | tf_op jit(solution)/shard_map/dot_general | solution.py:28
  107.6 0.1 collective-permute-start.3
  107.7 0.1 collective-permute-start.4
  107.8 0.1 collective-permute-start.5
  107.9 0.6 broadcast_in_dim.13
  108.5 3.6 %all-to-all-start = ((f32[4,1,2048]{2,1,0:T(1,128)}), f32[4,1,2048]{2,1,0:T(1,128)S(1)}, u32[]{:S(2)}, u32[]{:S(2)}) async-start(f32[4,1,2048]{2,1,0:T(1,128)} %broadcast_in_dim.13), calls=%async_computation | async-start | bytes 65536 | tf_op jit(solution)/shard_map/all_to_all | solution.py:17
  112.2 0.0 collective-permute-done.3
  112.2 0.0 collective-permute-done.4
  112.2 0.1 collective-permute-done.5
  112.2 0.6 maximum_maximum_fusion.1
  112.8 2.5 %all-to-all-done = f32[4,1,2048]{2,1,0:T(1,128)S(1)} async-done(((f32[4,1,2048]{2,1,0:T(1,128)}), f32[4,1,2048]{2,1,0:T(1,128)S(1)}, u32[]{:S(2)}, u32[]{:S(2)}) %all-to-all-start) | async-done | bytes 32800 | tf_op jit(solution)/shard_map/all_to_all | solution.py:17
  115.4 0.7 dynamic_slice.23
  (6 shorter events, 0.1 us)
Async XLA Ops:
  7.2 32.9 %copy-start.1 = (s32[131072]{0:T(1024)S(1)}, s32[131072]{0:T(1024)}, u32[]{:S(2)}) copy-start(s32[131072]{0:T(1024)} %param.3) | copy-start | bytes 1572868
  7.2 89.1 %all-gather.2.cloned.1.call-start = ((), (), s32[]{:S(2)}) async-start(), calls=%async_computation.1 | async-start | bytes 3932160 | tf_op jit(solution)/shard_map/all_gather | solution.py:45
  11.3 28.8 %collective-permute-start = (bf16[512,768]{1,0:T(8,128)(2,1)}, bf16[512,768]{1,0:T(8,128)(2,1)S(1)}, u32[]{:S(2)}, u32[]{:S(2)}) collective-permute-start(bf16[512,768]{1,0:T(8,128)(2,1)} %multiply_convert_fusion), channel_id=1, source_target_pairs={{0,4},{4,8},{8,12},{12,16},{16,20},{20,24},{24,28},{28,32},{32,36}... | collective-permute-start | bytes 2359304 | tf_op jit(solution)/shard_map/ppermute | solution.py:12
  40.1 23.5 %collective-permute-start.1 = (bf16[512,768]{1,0:T(8,128)(2,1)S(1)}, bf16[512,768]{1,0:T(8,128)(2,1)S(1)}, u32[]{:S(2)}, u32[]{:S(2)}) collective-permute-start(bf16[512,768]{1,0:T(8,128)(2,1)S(1)} %collective-permute-done), channel_id=1, source_target_pairs={{0,4},{4,8},{8,12},{12,16},{16,20},{20,24},{24,28},{28,32},{32,36}... | collective-permute-start | bytes 2359304 | tf_op jit(solution)/shard_map/ppermute | solution.py:12
  63.6 40.3 %collective-permute-start.2 = (bf16[512,768]{1,0:T(8,128)(2,1)S(1)}, bf16[512,768]{1,0:T(8,128)(2,1)S(1)}, u32[]{:S(2)}, u32[]{:S(2)}) collective-permute-start(bf16[512,768]{1,0:T(8,128)(2,1)S(1)} %collective-permute-done.1), channel_id=1, source_target_pairs={{0,4},{4,8},{8,12},{12,16},{16,20},{20,24},{24,28},{28,32},{32,36}... | collective-permute-start | bytes 2359304 | tf_op jit(solution)/shard_map/ppermute | solution.py:12
  96.3 3.9 %copy-start.2 = (bf16[2048,768]{1,0:T(8,128)(2,1)S(1)}, bf16[2048,768]{1,0:T(8,128)(2,1)}, u32[]{:S(2)}) copy-start(bf16[2048,768]{1,0:T(8,128)(2,1)} %all-gather.2.cloned.1.call-done) | copy-start | bytes 9437188
  100.2 1.9 %copy-start = (bf16[512,768]{1,0:T(8,128)(2,1)S(1)}, bf16[512,768]{1,0:T(8,128)(2,1)}, u32[]{:S(2)}) copy-start(bf16[512,768]{1,0:T(8,128)(2,1)} %multiply_convert_fusion) | copy-start | bytes 2359300
  102.0 1.9 %dynamic-slice-start = ((s32[131072]{0:T(1024)}, s32[]{:T(128)}), s32[2048]{0:T(1024)S(1)}, s32[]{:S(2)}) async-start(s32[131072]{0:T(1024)} %param.3, s32[]{:T(128)} %select_n.52), calls=%async_computation.2 | async-start | bytes 16896 | tf_op jit(solution)/shard_map/dynamic_slice | solution.py:46
  107.6 4.6 %collective-permute-start.3 = (f32[512]{0:T(512)S(1)}, f32[512]{0:T(512)S(1)}, u32[]{:S(2)}, u32[]{:S(2)}) collective-permute-start(f32[512]{0:T(512)S(1)} %get-tuple-element.2), channel_id=1, source_target_pairs={{0,252},{4,0},{8,4},{12,8},{16,12},{20,16},{24,20},{28,24},{32,28}... | collective-permute-start | bytes 6152 | tf_op jit(solution)/shard_map/ppermute | solution.py:12
  107.7 4.5 %collective-permute-start.4 = (f32[512]{0:T(512)S(1)}, f32[512]{0:T(512)S(1)}, u32[]{:S(2)}, u32[]{:S(2)}) collective-permute-start(f32[512]{0:T(512)S(1)} %get-tuple-element.13), channel_id=1, source_target_pairs={{0,248},{4,252},{8,0},{12,4},{16,8},{20,12},{24,16},{28,20},{32,24... | collective-permute-start | bytes 6152 | tf_op jit(solution)/shard_map/ppermute | solution.py:12
  107.8 4.4 %collective-permute-start.5 = (f32[512]{0:T(512)S(1)}, f32[512]{0:T(512)S(1)}, u32[]{:S(2)}, u32[]{:S(2)}) collective-permute-start(f32[512]{0:T(512)S(1)} %get-tuple-element.15), channel_id=1, source_target_pairs={{0,244},{4,248},{8,252},{12,0},{16,4},{20,8},{24,12},{28,16},{32,2... | collective-permute-start | bytes 6152 | tf_op jit(solution)/shard_map/ppermute | solution.py:12
  108.5 6.8 %all-to-all-start = ((f32[4,1,2048]{2,1,0:T(1,128)}), f32[4,1,2048]{2,1,0:T(1,128)S(1)}, u32[]{:S(2)}, u32[]{:S(2)}) async-start(f32[4,1,2048]{2,1,0:T(1,128)} %broadcast_in_dim.13), calls=%async_computation | async-start | bytes 65536 | tf_op jit(solution)/shard_map/all_to_all | solution.py:17
Sparse Core Ops, SparseCore 0:
  11.5 84.7 all-gather.1
where the time goes:
time: 125 us; the launch traced here: 123 us
  waiting for transfers between devices  84.9 us (68%)
  between operations  14.2 us (11%)
  matrix products  11.2 us (9%)
  starting transfers between devices  6.47 us (5%)
  other arithmetic  4.71 us (4%)
  local copies, waits for them, and re-layouts  1.38 us (1%)
    ppermute x6, waiting for transfers between devices, shifted(): return lax.ppermute(value, axis, pairs)  49.7 us
    all_gather x1, waiting for transfers between devices, shards(): host = lax.all_gather(unit, 'rep', axis=0, tiled=True)  32.7 us
    dot_general x4, matrix products, best_pair(): lax.dot_general(host, visit, (((1,), (1,)), ((), ())), preferred_element_...  11.2 us
    all_to_all x1, starting transfers between devices, from_everyone(): lax.all_to_all(jnp.broadcast_to(value[None], (peers, *value.shape)), axis...  3.64 us
    ppermute x6, starting transfers between devices, shifted(): return lax.ppermute(value, axis, pairs)  2.79 us
    all_to_all x1, waiting for transfers between devices, from_everyone(): lax.all_to_all(jnp.broadcast_to(value[None], (peers, *value.shape)), axis...  2.52 us
  transfers between devices with their start and end apart: 8, of which 5 were waited for; matrix products, arithmetic and copies ran while one was open for 7% of the time, Pallas kernels for 0%

commit v1 on v0

v1 whole, which is shorter than its diff:
```python
import functools

import jax
import jax.numpy as jnp
from jax import lax
from jax.experimental import pallas as pl
from jax.experimental.pallas import tpu as pltpu

MESH = pl.DeviceIdType.MESH
ROWS = 512
WIDTH = 768
CHUNKS = 8
PIECE = ROWS // CHUNKS
HALF = CHUNKS // 2
TILE = 256
LOW = -1.0

UP, UP2, DOWN, FAR, SIDE, PAIR, PAIR_SIDE, PAIR_DOWN, PAIR_FAR = range(9)


def kernel(
    blocks,
    emb_hbm,
    rank_hbm,
    early_ref,
    late_ref,
    emb,
    raw,
    host,
    visit,
    lane_rank,
    row_rank,
    host_best,
    visit_best,
    host_out,
    host_in,
    visit_out,
    visit_in,
    load_sem,
    rank_sem,
    send_sem,
    recv_sem,
    out_send,
    out_recv,
):
    b = lax.axis_index("blk")
    r = lax.axis_index("rep")
    y, c = r // 2, r % 2
    next_b, next_y = (b + 1) % blocks, (y + (b % 8) // 7) % 2
    prev_b, prev_y = (b + blocks - 1) % blocks, (y + (7 - b % 8) // 7) % 2
    back_b = (b + blocks - 2) % blocks
    back_y = (prev_y + (7 - prev_b % 8) // 7) % 2
    up = (next_b, next_y * 2 + c)
    down = (prev_b, prev_y * 2 + c)
    back = (back_b, back_y * 2 + c)
    side = (b, (1 - y) * 2 + c)
    pair = (b, y * 2 + 1 - c)

    def part(base_y, slot):
        return ((base_y + slot % 2) % 2) * 2 + (c + slot // 2) % 2

    def rows(i):
        return pl.ds(i * PIECE, PIECE)

    def copy(stream, i):
        own = host.at[0, rows(i)]
        mine_far = host.at[0, pl.ds(ROWS + i * PIECE, PIECE)]
        next_own = host.at[1, rows(i)]
        next_far = host.at[1, pl.ds(ROWS + i * PIECE, PIECE)]
        if stream == UP:
            src, dst, to = own, visit.at[0, rows(i)], up
        elif stream == UP2:
            src, dst, to = visit.at[0, rows(i)], visit.at[1, rows(i)], up
        elif stream == DOWN:
            src, dst, to = own, next_own, down
        elif stream == FAR and i < HALF:
            src, dst, to = next_own, next_far, side
        elif stream == FAR:
            src, dst, to = mine_far, next_far, down
        elif stream == SIDE:
            src, dst, to = own, mine_far, side
        elif stream == PAIR:
            src, dst, to = own, host.at[0, pl.ds(2 * ROWS + i * PIECE, PIECE)], pair
        elif stream == PAIR_SIDE:
            src, dst, to = mine_far, host.at[0, pl.ds(3 * ROWS + i * PIECE, PIECE)], pair
        elif stream == PAIR_DOWN:
            src, dst, to = next_own, host.at[1, pl.ds(2 * ROWS + i * PIECE, PIECE)], pair
        else:
            src, dst, to = next_far, host.at[1, pl.ds(3 * ROWS + i * PIECE, PIECE)], pair
        return pltpu.make_async_remote_copy(
            src_ref=src,
            dst_ref=dst,
            send_sem=send_sem.at[stream, i],
            recv_sem=recv_sem.at[stream, i],
            device_id=to,
            device_id_type=MESH,
        )

    started = []

    def send(stream, i):
        one = copy(stream, i)
        one.start()
        started.append(one)

    def arrived(stream, i):
        copy(stream, i).wait_recv()

    loads = [
        pltpu.make_async_copy(emb_hbm.at[rows(i)], emb.at[rows(i)], load_sem.at[i])
        for i in range(CHUNKS)
    ]
    for load in loads:
        load.start()
    rank_loads = [
        pltpu.make_async_copy(
            rank_hbm.at[pl.ds(pl.multiple_of(at * 16, 16), 16)], raw.at[k], rank_sem.at[k]
        )
        for k, at in enumerate((b, next_b, prev_b, back_b))
    ]
    for load in rank_loads:
        load.start()

    barrier = pltpu.get_barrier_semaphore()
    for to in (up, down, side, pair):
        pl.semaphore_signal(barrier, inc=1, device_id=to, device_id_type=MESH)

    host_best[...] = jnp.full_like(host_best, LOW)
    visit_best[...] = jnp.full_like(visit_best, LOW)

    def first(i):
        for stream in (UP, DOWN, SIDE, PAIR):
            send(stream, i)

    for i in range(CHUNKS):
        loads[i].wait()
        x = emb[rows(i), :]
        squares = jnp.sum(x * x, axis=1, keepdims=True)
        host[0, rows(i), :] = (x * lax.rsqrt(squares + 1e-06)).astype(jnp.bfloat16)
        if i == 0:
            pl.semaphore_wait(barrier, 4)
        else:
            first(i - 1)
    for load in rank_loads:
        load.wait()
    first(CHUNKS - 1)

    for k, base_y in ((0, y), (1, next_y)):
        for slot in range(4):
            lane_rank[k, pl.ds(slot * 4, 4), :] = raw[
                k, pl.ds(part(base_y, slot) * 4, 4), :
            ].astype(jnp.float32)
    for k, (at, base_y) in enumerate(((0, y), (2, prev_y), (3, back_y))):
        for t in range(4):
            line = raw[at, pl.ds(part(base_y, 0) * 4 + t, 1), :].astype(jnp.float32)
            row_rank[k, pl.ds(t * 128, 128), :] = jnp.broadcast_to(line, (128, 128)).T

    def meet(k, first_tile, tiles, who, start, count):
        source = host.at[0, pl.ds(0, ROWS)] if who == 0 else visit.at[who - 1]

        def one(j, carry):
            at = pl.multiple_of(j * TILE, TILE)
            scores = lax.dot_general(
                source[pl.ds(start, count), :],
                host[k, pl.ds(at, TILE), :],
                (((1,), (1,)), ((), ())),
                preferred_element_type=jnp.float32,
            )
            below = row_rank[who, pl.ds(start, count), :]
            best = visit_best[who, pl.ds(start, count), :]
            for t in range(TILE // 128):
                above = lane_rank[k, pl.ds(j * (TILE // 128) + t, 1), :]
                kept = jnp.where(below < above, scores[:, t * 128 : (t + 1) * 128], LOW)
                best = jnp.maximum(best, kept)
                over = jnp.max(kept.reshape(count // 8, 8, 128), axis=0)
                where = pl.ds(pl.multiple_of(at + t * 128, 128), 128)
                host_best[k, :, where] = jnp.maximum(host_best[k, :, where], over)
            visit_best[who, pl.ds(start, count), :] = best
            return carry

        lax.fori_loop(first_tile, first_tile + tiles, one, 0)

    meet(0, 0, 2, 0, 0, ROWS)
    for i in range(CHUNKS):
        arrived(PAIR, i)
    meet(0, 4, 2, 0, 0, ROWS)
    for i in range(CHUNKS):
        arrived(SIDE, i)
        send(PAIR_SIDE, i)
        arrived(DOWN, i)
        send(PAIR_DOWN, i)
        if i < HALF:
            send(FAR, i)
        arrived(UP, i)
        send(UP2, i)
        if i >= HALF:
            send(FAR, i)
        if i == HALF - 1:
            meet(0, 2, 1, 0, 0, ROWS)
        if i == HALF:
            for n in range(HALF):
                arrived(PAIR_SIDE, n)
            meet(0, 6, 1, 0, 0, ROWS)
    for i in range(HALF, CHUNKS):
        arrived(PAIR_SIDE, i)
    for i in range(CHUNKS):
        arrived(PAIR_DOWN, i)
    for i in range(HALF):
        arrived(FAR, i)
        send(PAIR_FAR, i)
        arrived(FAR, i + HALF)
        send(PAIR_FAR, i + HALF)
        if i == 0:
            meet(0, 3, 1, 0, 0, ROWS)
            meet(0, 7, 1, 0, 0, ROWS)
        else:
            meet(0, (i - 1) * 3, 3 if i < 3 else 2, 1, 0, ROWS)
    meet(1, 0, 2, 1, 0, ROWS)
    meet(1, 4, 2, 1, 0, ROWS)
    for i in range(CHUNKS):
        arrived(PAIR_FAR, i)
    meet(1, 2, 2, 1, 0, ROWS)
    meet(1, 6, 2, 1, 0, ROWS)

    def host_result(k):
        for n in range(16):
            host_out[k, n // 4, pl.ds(n % 4, 1), :] = jnp.max(
                host_best[k, :, pl.ds(n * 128, 128)], axis=0, keepdims=True
            )

    def visit_result(who):
        for t in range(4):
            visit_out[who, pl.ds(t, 1), :] = jnp.max(
                visit_best[who, pl.ds(t * 128, 128), :].T, axis=0, keepdims=True
            )

    def host_copy(k, slot):
        return pltpu.make_async_remote_copy(
            src_ref=host_out.at[k, slot],
            dst_ref=host_in.at[k, slot],
            send_sem=out_send.at[k * 4 + slot],
            recv_sem=out_recv.at[k * 4 + slot],
            device_id=(b, part(y, slot)) if k == 0 else (next_b, part(next_y, slot)),
            device_id_type=MESH,
        )

    def visit_copy(who):
        return pltpu.make_async_remote_copy(
            src_ref=visit_out.at[who],
            dst_ref=visit_in.at[who],
            send_sem=out_send.at[8 + who],
            recv_sem=out_recv.at[8 + who],
            device_id=down if who == 1 else back,
            device_id_type=MESH,
        )

    results = []

    def give(one):
        one.start()
        results.append(one)

    host_result(0)
    visit_result(1)
    visit_result(0)
    for slot in range(1, 4):
        give(host_copy(0, slot))
    give(visit_copy(1))

    for i in range(HALF):
        arrived(UP2, i)
    meet(1, 0, 8, 2, 0, HALF * PIECE)
    for i in range(HALF, CHUNKS):
        arrived(UP2, i)
        meet(1, 0, 8, 2, i * PIECE, PIECE)
    host_result(1)
    visit_result(2)
    for slot in range(4):
        give(host_copy(1, slot))
    give(visit_copy(2))

    for one in started:
        one.wait_send()
    for one in results:
        one.wait_recv()
    early = host_out[0, 0]
    for slot in range(1, 4):
        early = jnp.maximum(early, host_in[0, slot])
    for slot in range(4):
        early = jnp.maximum(early, host_in[1, slot])
    early_ref[...] = early
    late_ref[...] = jnp.maximum(visit_out[0], jnp.maximum(visit_in[1], visit_in[2]))
    for one in results:
        one.wait_send()


def shards(blocks, embeddings, ranks):
    out = jax.ShapeDtypeStruct((4, 128), jnp.float32)
    early, late = pl.pallas_call(
        functools.partial(kernel, blocks),
        out_shape=(out, out),
        in_specs=[pl.BlockSpec(memory_space=pl.ANY)] * 2,
        out_specs=(pl.BlockSpec(memory_space=pltpu.VMEM),) * 2,
        scratch_shapes=[
            pltpu.VMEM((ROWS, WIDTH), jnp.float32),
            pltpu.VMEM((4, 16, 128), jnp.int32),
            pltpu.VMEM((2, 4 * ROWS, WIDTH), jnp.bfloat16),
            pltpu.VMEM((2, ROWS, WIDTH), jnp.bfloat16),
            pltpu.VMEM((2, 16, 128), jnp.float32),
            pltpu.VMEM((3, ROWS, 128), jnp.float32),
            pltpu.VMEM((2, 8, 4 * ROWS), jnp.float32),
            pltpu.VMEM((3, ROWS, 128), jnp.float32),
            pltpu.VMEM((2, 4, 4, 128), jnp.float32),
            pltpu.VMEM((2, 4, 4, 128), jnp.float32),
            pltpu.VMEM((3, 4, 128), jnp.float32),
            pltpu.VMEM((3, 4, 128), jnp.float32),
            pltpu.SemaphoreType.DMA((CHUNKS,)),
            pltpu.SemaphoreType.DMA((4,)),
            pltpu.SemaphoreType.DMA((9, CHUNKS)),
            pltpu.SemaphoreType.DMA((9, CHUNKS)),
            pltpu.SemaphoreType.DMA((11,)),
            pltpu.SemaphoreType.DMA((11,)),
        ],
        compiler_params=pltpu.CompilerParams(
            collective_id=0, has_side_effects=True, vmem_limit_bytes=40 << 20
        ),
    )(embeddings, ranks.reshape(-1, 128))
    return early.reshape(-1), late.reshape(-1)


def solution(mesh):
    from jax.sharding import PartitionSpec as P

    return jax.shard_map(
        functools.partial(shards, mesh.shape["blk"]),
        mesh=mesh,
        in_specs=(P(("blk", "rep"), None), P()),
        out_specs=(P(("blk", "rep")), P(("blk", "rep"))),
        check_vma=False,
    )
```

time: 125 us -> 70.5 us (0.56); the launches traced: 123 us -> 70.3 us
  waiting for transfers between devices: 84.9 us -> 0 us
  Pallas kernels: 0 us -> 66.1 us
  between operations: 14.2 us -> 0.65 us
  matrix products: 11.2 us -> 0 us
  starting transfers between devices: 6.47 us -> 0 us
  other arithmetic: 4.71 us -> 0 us
  local copies, waits for them, and re-layouts: 1.38 us -> 3.6 us
    pallas_call x0 -> x1, Pallas kernels: none -> 66.1 us  [shards(): pl.pallas_call(functools.partial(kernel, blocks), out_shape=(out, out), i...]
    ppermute x6 -> x0, waiting for transfers between devices: 49.7 us -> none  [shifted(): return lax.ppermute(value, axis, pairs)]
    all_gather x1 -> x0, waiting for transfers between devices: 32.7 us -> none  [shards(): host = lax.all_gather(unit, 'rep', axis=0, tiled=True)]
    dot_general x4 -> x0, matrix products: 11.2 us -> none  [best_pair(): lax.dot_general(host, visit, (((1,), (1,)), ((), ())), preferred_element_...]
    all_to_all x1 -> x0, starting transfers between devices: 3.64 us -> none  [from_everyone(): lax.all_to_all(jnp.broadcast_to(value[None], (peers, *value.shape)), axis...]
    unnamed x6, local copies, waits for them, and re-layouts: 0.01 us -> 3.6 us
    ppermute x6 -> x0, starting transfers between devices: 2.79 us -> none  [shifted(): return lax.ppermute(value, axis, pairs)]
    all_to_all x1 -> x0, waiting for transfers between devices: 2.52 us -> none  [from_everyone(): lax.all_to_all(jnp.broadcast_to(value[None], (peers, *value.shape)), axis...]
  transfers between devices with their start and end apart: 8 -> 0, of which waited for: 5 -> 0; matrix products, arithmetic and copies ran while one was open for 7% -> 0% of each run, Pallas kernels for 0% -> 0%
where the time goes in v1:
time: 70.5 us; the launch traced here: 70.3 us
  Pallas kernels  66.1 us (94%)
  local copies, waits for them, and re-layouts  3.6 us (5%)
    pallas_call x1, Pallas kernels, shards(): pl.pallas_call(functools.partial(kernel, blocks), out_shape=(out, out), i...  66.1 us
    unnamed x6, local copies, waits for them, and re-layouts  3.6 us

profile of v1, /device:TPU:1, one launch (start us, length us, event | category | flops | bytes accessed | tf_op | source)
XLA Modules:
  0.0 70.3 jit_solution(12410701436396225210)
XLA Ops:
  0.6 0.0 copy-start
  0.6 1.4 %copy-done = f32[512,768]{1,0:T(8,128)S(1)} copy-done((f32[512,768]{1,0:T(8,128)S(1)}, f32[512,768]{1,0:T(8,128)}, u32[]{:S(2)}) %copy-start) | copy-done | bytes 1572888
  2.0 0.0 copy-start.1
  2.0 1.0 %copy-done.1 = s32[131072]{0:T(1024)S(1)} copy-done((s32[131072]{0:T(1024)S(1)}, s32[131072]{0:T(1024)}, u32[]{:S(2)}) %copy-start.1) | copy-done | bytes 524312
  3.1 66.1 %shard_map.41 = (f32[4,128]{1,0:T(4,128)S(1)}, f32[4,128]{1,0:T(4,128)S(1)}) custom-call(f32[512,768]{1,0:T(8,128)S(1)} %copy-done, s32[1024,128]{1,0:T(8,128)S(1)} %bitcast.3), custom_call_target="tpu_custom_call" | custom-call | tf_op jit(solution)/shard_map/pallas_call | solution.py:299
  69.1 0.6 copy.6
  69.7 0.6 copy.7
Async XLA Ops:
  0.6 1.4 %copy-start = (f32[512,768]{1,0:T(8,128)S(1)}, f32[512,768]{1,0:T(8,128)}, u32[]{:S(2)}) copy-start(f32[512,768]{1,0:T(8,128)} %emb_hbm.1) | copy-start | bytes 4718596
  2.0 1.0 %copy-start.1 = (s32[131072]{0:T(1024)S(1)}, s32[131072]{0:T(1024)}, u32[]{:S(2)}) copy-start(s32[131072]{0:T(1024)} %param.3) | copy-start | bytes 1572868

commit v2 on v1

--- a/solution.py
+++ b/solution.py
@@ -46,10 +46,9 @@
     b = lax.axis_index("blk")
     r = lax.axis_index("rep")
     y, c = r // 2, r % 2
-    next_b, next_y = (b + 1) % blocks, (y + (b % 8) // 7) % 2
-    prev_b, prev_y = (b + blocks - 1) % blocks, (y + (7 - b % 8) // 7) % 2
-    back_b = (b + blocks - 2) % blocks
-    back_y = (prev_y + (7 - prev_b % 8) // 7) % 2
+    next_b, next_y = (b + blocks - 1) % blocks, (y + (7 - b % 8) // 7) % 2
+    prev_b, prev_y = (b + 1) % blocks, (y + (b % 8) // 7) % 2
+    back_b, back_y = (b + 2) % blocks, (prev_y + (prev_b % 8) // 7) % 2
     up = (next_b, next_y * 2 + c)
     down = (prev_b, prev_y * 2 + c)
     back = (back_b, back_y * 2 + c)
@@ -170,7 +169,7 @@
             best = visit_best[who, pl.ds(start, count), :]
             for t in range(TILE // 128):
                 above = lane_rank[k, pl.ds(j * (TILE // 128) + t, 1), :]
-                kept = jnp.where(below < above, scores[:, t * 128 : (t + 1) * 128], LOW)
+                kept = jnp.where(above < below, scores[:, t * 128 : (t + 1) * 128], LOW)
                 best = jnp.maximum(best, kept)
                 over = jnp.max(kept.reshape(count // 8, 8, 128), axis=0)
                 where = pl.ds(pl.multiple_of(at + t * 128, 128), 128)
@@ -283,13 +282,13 @@
         one.wait_send()
     for one in results:
         one.wait_recv()
-    early = host_out[0, 0]
+    late = host_out[0, 0]
     for slot in range(1, 4):
-        early = jnp.maximum(early, host_in[0, slot])
+        late = jnp.maximum(late, host_in[0, slot])
     for slot in range(4):
-        early = jnp.maximum(early, host_in[1, slot])
-    early_ref[...] = early
-    late_ref[...] = jnp.maximum(visit_out[0], jnp.maximum(visit_in[1], visit_in[2]))
+        late = jnp.maximum(late, host_in[1, slot])
+    late_ref[...] = late
+    early_ref[...] = jnp.maximum(visit_out[0], jnp.maximum(visit_in[1], visit_in[2]))
     for one in results:
         one.wait_send()
 
@@ -299,7 +298,7 @@
     early, late = pl.pallas_call(
         functools.partial(kernel, blocks),
         out_shape=(out, out),
-        in_specs=[pl.BlockSpec(memory_space=pl.ANY)] * 2,
+        in_specs=[pl.BlockSpec(memory_space=pltpu.HBM)] * 2,
         out_specs=(pl.BlockSpec(memory_space=pltpu.VMEM),) * 2,
         scratch_shapes=[
             pltpu.VMEM((ROWS, WIDTH), jnp.float32),

time: 70.5 us -> 65.5 us (0.929)
  Pallas kernels: 66.1 us -> 60.7 us
    pallas_call x1, Pallas kernels: 66.1 us -> 60.7 us  [shards(): pl.pallas_call(functools.partial(kernel, blocks), out_shape=(out, out), i...]
where the time goes in v2:
time: 65.5 us; the launch traced here: 64.9 us
  Pallas kernels  60.7 us (93%)
  local copies, waits for them, and re-layouts  3.6 us (5%)
    pallas_call x1, Pallas kernels, shards(): pl.pallas_call(functools.partial(kernel, blocks), out_shape=(out, out), i...  60.7 us
    unnamed x6, local copies, waits for them, and re-layouts  3.6 us

profile of v2, /device:TPU:1, one launch (start us, length us, event | category | flops | bytes accessed | tf_op | source)
XLA Modules:
  0.0 64.9 jit_solution(10030094050928194661)
XLA Ops:
  0.6 0.0 copy-start
  0.6 1.4 %copy-done = f32[512,768]{1,0:T(8,128)S(1)} copy-done((f32[512,768]{1,0:T(8,128)S(1)}, f32[512,768]{1,0:T(8,128)}, u32[]{:S(2)}) %copy-start) | copy-done | bytes 1572888
  2.0 0.0 copy-start.1
  2.0 1.0 %copy-done.1 = s32[131072]{0:T(1024)S(1)} copy-done((s32[131072]{0:T(1024)S(1)}, s32[131072]{0:T(1024)}, u32[]{:S(2)}) %copy-start.1) | copy-done | bytes 524312
  3.1 60.7 %shard_map.41 = (f32[4,128]{1,0:T(4,128)S(1)}, f32[4,128]{1,0:T(4,128)S(1)}) custom-call(f32[512,768]{1,0:T(8,128)S(1)} %copy-done, s32[1024,128]{1,0:T(8,128)S(1)} %bitcast.3), custom_call_target="tpu_custom_call" | custom-call | tf_op jit(solution)/shard_map/pallas_call | solution.py:298
  63.8 0.6 copy.6
  64.4 0.6 copy.7
Async XLA Ops:
  0.6 1.4 %copy-start = (f32[512,768]{1,0:T(8,128)S(1)}, f32[512,768]{1,0:T(8,128)}, u32[]{:S(2)}) copy-start(f32[512,768]{1,0:T(8,128)} %emb_hbm.1) | copy-start | bytes 4718596
  2.0 1.0 %copy-start.1 = (s32[131072]{0:T(1024)S(1)}, s32[131072]{0:T(1024)}, u32[]{:S(2)}) copy-start(s32[131072]{0:T(1024)} %param.3) | copy-start | bytes 1572868

commit v3 on v2

v3 whole, which is shorter than its diff:
```python
import functools

import jax
import jax.numpy as jnp
from jax import lax
from jax.experimental import pallas as pl
from jax.experimental.pallas import tpu as pltpu
from jax.sharding import PartitionSpec as P

MESH = pl.DeviceIdType.MESH
ROWS = 512
WIDTH = 768
PIECES = 8
PIECE = ROWS // PIECES
LANES = 128
CHUNKS = ROWS // LANES
HALF = CHUNKS // 2
LOW = -1.0

VIS, VIS2, UP, FAR, SIDE, PAIR, PAIR_SIDE, PAIR_UP, PAIR_FAR = range(9)


def kernel(
    blocks,
    emb_hbm,
    rank_hbm,
    late_ref,
    early_ref,
    emb,
    raw,
    host,
    visit,
    lane_rank,
    row_rank,
    host_best,
    visit_best,
    host_out,
    host_in,
    visit_out,
    visit_in,
    load_sem,
    rank_sem,
    send_sem,
    recv_sem,
    out_send,
    out_recv,
):
    b = lax.axis_index("blk")
    r = lax.axis_index("rep")
    y, c = r // 2, r % 2
    low_b, low_y = (b + blocks - 1) % blocks, (y + (7 - b % 8) // 7) % 2
    high_b, high_y = (b + 1) % blocks, (y + (b % 8) // 7) % 2
    top_b, top_y = (b + 2) % blocks, (high_y + (high_b % 8) // 7) % 2
    low = (low_b, low_y * 2 + c)
    high = (high_b, high_y * 2 + c)
    top = (top_b, top_y * 2 + c)
    side = (b, (1 - y) * 2 + c)
    pair = (b, y * 2 + 1 - c)

    def part(base_y, slot):
        return ((base_y + slot // 2) % 2) * 2 + (c + slot % 2) % 2

    def rows(i):
        return pl.ds(i * PIECE, PIECE)

    def copy(stream, i):
        if stream == VIS:
            src, dst, to = visit.at[0, rows(i)], visit.at[1, rows(i)], low
        elif stream == VIS2:
            src, dst, to = visit.at[1, rows(i)], visit.at[2, rows(i)], low
        elif stream == UP:
            src, dst, to = host.at[0, i], host.at[1, i], high
        elif stream == FAR and i < HALF:
            src, dst, to = host.at[1, i], host.at[1, 2 * CHUNKS + i], side
        elif stream == FAR:
            src, dst, to = host.at[0, 2 * CHUNKS + i], host.at[1, 2 * CHUNKS + i], high
        elif stream == SIDE:
            src, dst, to = host.at[0, i], host.at[0, 2 * CHUNKS + i], side
        else:
            k = 0 if stream in (PAIR, PAIR_SIDE) else 1
            at = i if stream in (PAIR, PAIR_UP) else 2 * CHUNKS + i
            src, dst, to = host.at[k, at], host.at[k, at + CHUNKS], pair
        return pltpu.make_async_remote_copy(
            src_ref=src,
            dst_ref=dst,
            send_sem=send_sem.at[stream, i],
            recv_sem=recv_sem.at[stream, i],
            device_id=to,
            device_id_type=MESH,
        )

    started = []

    def send(stream, i):
        one = copy(stream, i)
        one.start()
        started.append(one)

    def arrived(stream, i):
        copy(stream, i).wait_recv()

    loads = [
        pltpu.make_async_copy(emb_hbm.at[rows(i)], emb.at[rows(i)], load_sem.at[i])
        for i in range(PIECES)
    ]
    for load in loads:
        load.start()

    barrier = pltpu.get_barrier_semaphore()
    for to in (low, high, side, pair):
        pl.semaphore_signal(barrier, inc=1, device_id=to, device_id_type=MESH)

    rank_loads = [
        pltpu.make_async_copy(
            rank_hbm.at[pl.ds(pl.multiple_of(at * 16, 16), 16)], raw.at[k], rank_sem.at[k]
        )
        for k, at in enumerate((b, low_b, high_b, top_b))
    ]
    for load in rank_loads:
        load.start()

    host_best[...] = jnp.full_like(host_best, LOW)
    visit_best[...] = jnp.full_like(visit_best, LOW)

    def first(j):
        for stream in (UP, SIDE, PAIR):
            send(stream, j)

    for j in range(CHUNKS):
        group = []
        for i in (2 * j, 2 * j + 1):
            loads[i].wait()
            x = emb[rows(i), :]
            squares = jnp.sum(x * x, axis=1, keepdims=True)
            unit = x * lax.rsqrt(squares + 1e-06)
            visit[0, rows(i), :] = unit.astype(jnp.bfloat16)
            group.append(unit)
            if i == 0:
                pl.semaphore_wait(barrier, 4)
            else:
                send(VIS, i - 1)
        host[0, j] = jnp.concatenate(group, axis=0).T.astype(jnp.bfloat16)
        if j:
            first(j - 1)
    send(VIS, PIECES - 1)
    for load in rank_loads:
        load.wait()
    first(CHUNKS - 1)

    for k, base_y in ((0, y), (1, low_y)):
        for slot in range(4):
            lane_rank[k, pl.ds(slot * 4, 4), :] = raw[
                k, pl.ds(part(base_y, slot) * 4, 4), :
            ].astype(jnp.float32)
    for k, (at, base_y) in enumerate(((0, y), (2, high_y), (3, top_y))):
        for t in range(4):
            line = raw[at, pl.ds(part(base_y, 0) * 4 + t, 1), :].astype(jnp.float32)
            row_rank[k, pl.ds(t * 128, 128), :] = jnp.broadcast_to(line, (128, 128)).T

    def meet(k, chunk, chunks, who, start, count):
        scores = jnp.dot(
            visit[who, pl.ds(start, count), :],
            jnp.concatenate([host[k, chunk + n] for n in range(chunks)], axis=1),
            preferred_element_type=jnp.float32,
        )
        after = row_rank[who, pl.ds(start, count), :]
        best = visit_best[who, pl.ds(start, count), :]
        for n in range(chunks):
            before = lane_rank[k, pl.ds(chunk + n, 1), :]
            kept = jnp.where(before < after, scores[:, n * LANES : (n + 1) * LANES], LOW)
            best = jnp.maximum(best, kept)
            over = jnp.max(kept.reshape(count // 8, 8, LANES), axis=0)
            host_best[k, chunk + n] = jnp.maximum(host_best[k, chunk + n], over)
        visit_best[who, pl.ds(start, count), :] = best

    def half(k, which, who, start=0, count=ROWS):
        meet(k, which * 2 * CHUNKS, 2 * CHUNKS, who, start, count)

    def host_result(k):
        for n in range(4 * CHUNKS):
            host_out[k, n // CHUNKS, pl.ds(n % CHUNKS, 1), :] = jnp.max(
                host_best[k, n], axis=0, keepdims=True
            )

    def visit_result(who, t):
        visit_out[who, pl.ds(t, 1), :] = jnp.max(
            visit_best[who, pl.ds(t * 128, 128), :].T, axis=0, keepdims=True
        )

    def host_copy(k, slot):
        return pltpu.make_async_remote_copy(
            src_ref=host_out.at[k, slot],
            dst_ref=host_in.at[k, slot],
            send_sem=out_send.at[k * 4 + slot],
            recv_sem=out_recv.at[k * 4 + slot],
            device_id=(b, part(y, slot)) if k == 0 else (low_b, part(low_y, slot)),
            device_id_type=MESH,
        )

    def visit_copy(who):
        return pltpu.make_async_remote_copy(
            src_ref=visit_out.at[who],
            dst_ref=visit_in.at[who],
            send_sem=out_send.at[8 + who],
            recv_sem=out_recv.at[8 + who],
            device_id=high if who == 1 else top,
            device_id_type=MESH,
        )

    results = []

    def give(one):
        one.start()
        results.append(one)

    for j in range(CHUNKS):
        arrived(PAIR, j)
    half(0, 0, 0)
    for j in range(CHUNKS):
        for i in (2 * j, 2 * j + 1):
            arrived(VIS, i)
            send(VIS2, i)
        arrived(SIDE, j)
        send(PAIR_SIDE, j)
        if j >= HALF:
            send(FAR, j)
        arrived(UP, j)
        send(PAIR_UP, j)
        if j < HALF:
            send(FAR, j)
    half(0, 0, 1)
    for j in range(CHUNKS):
        arrived(PAIR_SIDE, j)
    half(0, 1, 0)
    half(0, 1, 1)
    for j in range(CHUNKS):
        arrived(PAIR_UP, j)
    half(1, 0, 1)
    for j in range(HALF):
        for n in (j, j + HALF):
            arrived(FAR, n)
            send(PAIR_FAR, n)
    host_result(0)
    for t in range(4):
        visit_result(0, t)
    for slot in range(1, 4):
        give(host_copy(0, slot))
    for j in range(CHUNKS):
        arrived(PAIR_FAR, j)
    half(1, 1, 1)
    for t in range(4):
        visit_result(1, t)
    for i in range(PIECES // 2):
        arrived(VIS2, i)
    give(visit_copy(1))
    half(1, 0, 2, 0, ROWS // 2)
    half(1, 1, 2, 0, ROWS // 2)
    for i in (4, 5):
        arrived(VIS2, i)
    half(1, 0, 2, 4 * PIECE, 2 * PIECE)
    half(1, 1, 2, 4 * PIECE, 2 * PIECE)
    for t in range(3):
        visit_result(2, t)
    for i in (6, 7):
        arrived(VIS2, i)
        meet(1, 0, 4 * CHUNKS, 2, i * PIECE, PIECE)
    host_result(1)
    visit_result(2, 3)
    for slot in range(4):
        give(host_copy(1, slot))
    give(visit_copy(2))

    for one in started:
        one.wait_send()
    for one in results:
        one.wait_recv()
    late = host_out[0, 0]
    for slot in range(1, 4):
        late = jnp.maximum(late, host_in[0, slot])
    late_ref[0] = late
    late = host_in[1, 0]
    for slot in range(1, 4):
        late = jnp.maximum(late, host_in[1, slot])
    late_ref[1] = late
    early_ref[0] = jnp.maximum(visit_out[0], visit_in[1])
    early_ref[1] = visit_in[2]
    for one in results:
        one.wait_send()


def shards(blocks, embeddings, ranks):
    out = jax.ShapeDtypeStruct((2, 4, 128), jnp.float32)
    late, early = pl.pallas_call(
        functools.partial(kernel, blocks),
        out_shape=(out, out),
        in_specs=[pl.BlockSpec(memory_space=pltpu.HBM)] * 2,
        out_specs=(pl.BlockSpec(memory_space=pltpu.VMEM),) * 2,
        scratch_shapes=[
            pltpu.VMEM((ROWS, WIDTH), jnp.float32),
            pltpu.VMEM((4, 16, 128), jnp.int32),
            pltpu.VMEM((2, 4 * CHUNKS, WIDTH, LANES), jnp.bfloat16),
            pltpu.VMEM((3, ROWS, WIDTH), jnp.bfloat16),
            pltpu.VMEM((2, 16, 128), jnp.float32),
            pltpu.VMEM((3, ROWS, 128), jnp.float32),
            pltpu.VMEM((2, 4 * CHUNKS, 8, LANES), jnp.float32),
            pltpu.VMEM((3, ROWS, 128), jnp.float32),
            pltpu.VMEM((2, 4, 4, 128), jnp.float32),
            pltpu.VMEM((2, 4, 4, 128), jnp.float32),
            pltpu.VMEM((3, 4, 128), jnp.float32),
            pltpu.VMEM((3, 4, 128), jnp.float32),
            pltpu.SemaphoreType.DMA((PIECES,)),
            pltpu.SemaphoreType.DMA((4,)),
            pltpu.SemaphoreType.DMA((9, PIECES)),
            pltpu.SemaphoreType.DMA((9, PIECES)),
            pltpu.SemaphoreType.DMA((11,)),
            pltpu.SemaphoreType.DMA((11,)),
        ],
        compiler_params=pltpu.CompilerParams(
            collective_id=0, has_side_effects=True, vmem_limit_bytes=67043328 - (256 << 10)
        ),
    )(embeddings, ranks.reshape(-1, 128))

    def higher(one, other):
        return (jnp.maximum(one[0], other[0]), jnp.maximum(one[1], other[1]))

    start = jnp.float32(LOW)
    late, early = lax.reduce(
        (late.reshape(2, -1), early.reshape(2, -1)), (start, start), higher, (0,)
    )
    return early, late


def solution(mesh):
    return jax.shard_map(
        functools.partial(shards, mesh.shape["blk"]),
        mesh=mesh,
        in_specs=(P(("blk", "rep"), None), P()),
        out_specs=(P(("blk", "rep")), P(("blk", "rep"))),
        check_vma=False,
    )
```

time: 65.5 us -> 58.5 us (0.89)
  the two profiles are of different devices: /device:TPU:1 before, /device:TPU:32 now
where the time goes in v3:
time: 58.5 us; the launch traced here: 58.4 us
  Pallas kernels  56.5 us (97%)
  other arithmetic  1.29 us (2%)
  between operations  0.64 us (1%)
    pallas_call x1, Pallas kernels, shards(): pl.pallas_call(functools.partial(kernel, blocks), out_shape=(out, out), i...  56.5 us
    another operation x1, other arithmetic, shards(): lax.reduce((late.reshape(2, -1), early.reshape(2, -1)), (start, start), h...  1.29 us

profile of v3, /device:TPU:32, one launch (start us, length us, event | category | flops | bytes accessed | tf_op | source)
XLA Modules:
  0.0 58.4 jit_solution(5065130886330595498)
XLA Ops:
  0.6 56.5 %shard_map.41 = (f32[2,4,128]{2,1,0:T(4,128)}, f32[2,4,128]{2,1,0:T(4,128)}) custom-call(f32[512,768]{1,0:T(8,128)} %emb_hbm.1, s32[1024,128]{1,0:T(8,128)} %bitcast.7), custom_call_target="tpu_custom_call" | custom-call | tf_op jit(solution)/shard_map/pallas_call | solution.py:293
  57.1 1.3 %bitcast_reduce_fusion = (f32[512]{0:T(512)}, f32[512]{0:T(512)}) fusion(f32[1,2,4,128]{3,2,1,0:T(4,128)} %bitcast.9, f32[1,2,4,128]{3,2,1,0:T(4,128)} %bitcast.8), kind=kLoop, calls=%fused_computation | loop fusion | flops 1024 | bytes 12288 | tf_op jit(solution)/shard_map/reduce | solution.py:327

commit v4 on v3

--- a/solution.py
+++ b/solution.py
@@ -24,8 +24,8 @@
     blocks,
     emb_hbm,
     rank_hbm,
+    early_ref,
     late_ref,
-    early_ref,
     emb,
     raw,
     host,
@@ -42,18 +42,19 @@
     rank_sem,
     send_sem,
     recv_sem,
+    ready,
     out_send,
     out_recv,
 ):
     b = lax.axis_index("blk")
     r = lax.axis_index("rep")
     y, c = r // 2, r % 2
-    low_b, low_y = (b + blocks - 1) % blocks, (y + (7 - b % 8) // 7) % 2
-    high_b, high_y = (b + 1) % blocks, (y + (b % 8) // 7) % 2
-    top_b, top_y = (b + 2) % blocks, (high_y + (high_b % 8) // 7) % 2
-    low = (low_b, low_y * 2 + c)
-    high = (high_b, high_y * 2 + c)
-    top = (top_b, top_y * 2 + c)
+    next_b, next_y = (b + 1) % blocks, (y + (b % 8) // 7) % 2
+    prev_b, prev_y = (b + blocks - 1) % blocks, (y + (7 - b % 8) // 7) % 2
+    back_b, back_y = (b + blocks - 2) % blocks, (prev_y + (7 - prev_b % 8) // 7) % 2
+    ahead = (next_b, next_y * 2 + c)
+    behind = (prev_b, prev_y * 2 + c)
+    back = (back_b, back_y * 2 + c)
     side = (b, (1 - y) * 2 + c)
     pair = (b, y * 2 + 1 - c)
 
@@ -65,15 +66,15 @@
 
     def copy(stream, i):
         if stream == VIS:
-            src, dst, to = visit.at[0, rows(i)], visit.at[1, rows(i)], low
+            src, dst, to = visit.at[0, rows(i)], visit.at[1, rows(i)], ahead
         elif stream == VIS2:
-            src, dst, to = visit.at[1, rows(i)], visit.at[2, rows(i)], low
+            src, dst, to = visit.at[1, rows(i)], visit.at[2, rows(i)], ahead
         elif stream == UP:
-            src, dst, to = host.at[0, i], host.at[1, i], high
+            src, dst, to = host.at[0, i], host.at[1, i], behind
         elif stream == FAR and i < HALF:
             src, dst, to = host.at[1, i], host.at[1, 2 * CHUNKS + i], side
         elif stream == FAR:
-            src, dst, to = host.at[0, 2 * CHUNKS + i], host.at[1, 2 * CHUNKS + i], high
+            src, dst, to = host.at[0, 2 * CHUNKS + i], host.at[1, 2 * CHUNKS + i], behind
         elif stream == SIDE:
             src, dst, to = host.at[0, i], host.at[0, 2 * CHUNKS + i], side
         else:
@@ -107,14 +108,14 @@
         load.start()
 
     barrier = pltpu.get_barrier_semaphore()
-    for to in (low, high, side, pair):
+    for to in (behind, side, pair):
         pl.semaphore_signal(barrier, inc=1, device_id=to, device_id_type=MESH)
 
     rank_loads = [
         pltpu.make_async_copy(
             rank_hbm.at[pl.ds(pl.multiple_of(at * 16, 16), 16)], raw.at[k], rank_sem.at[k]
         )
-        for k, at in enumerate((b, low_b, high_b, top_b))
+        for k, at in enumerate((b, next_b, prev_b, back_b))
     ]
     for load in rank_loads:
         load.start()
@@ -123,7 +124,7 @@
     visit_best[...] = jnp.full_like(visit_best, LOW)
 
     def first(j):
-        for stream in (UP, SIDE, PAIR):
+        for stream in (SIDE, PAIR):
             send(stream, j)
 
     for j in range(CHUNKS):
@@ -136,7 +137,8 @@
             visit[0, rows(i), :] = unit.astype(jnp.bfloat16)
             group.append(unit)
             if i == 0:
-                pl.semaphore_wait(barrier, 4)
+                pl.semaphore_wait(barrier, 3)
+                pl.semaphore_signal(ready, inc=1, device_id=ahead, device_id_type=MESH)
             else:
                 send(VIS, i - 1)
         host[0, j] = jnp.concatenate(group, axis=0).T.astype(jnp.bfloat16)
@@ -146,16 +148,19 @@
     for load in rank_loads:
         load.wait()
     first(CHUNKS - 1)
-
-    for k, base_y in ((0, y), (1, low_y)):
+    for k, base_y in ((0, y), (1, next_y)):
         for slot in range(4):
             lane_rank[k, pl.ds(slot * 4, 4), :] = raw[
                 k, pl.ds(part(base_y, slot) * 4, 4), :
             ].astype(jnp.float32)
-    for k, (at, base_y) in enumerate(((0, y), (2, high_y), (3, top_y))):
+    for k, (at, base_y) in enumerate(((0, y), (2, prev_y), (3, back_y))):
         for t in range(4):
             line = raw[at, pl.ds(part(base_y, 0) * 4 + t, 1), :].astype(jnp.float32)
             row_rank[k, pl.ds(t * 128, 128), :] = jnp.broadcast_to(line, (128, 128)).T
+
+    pl.semaphore_wait(ready, 1)
+    for j in range(CHUNKS):
+        send(UP, j)
 
     def meet(k, chunk, chunks, who, start, count):
         scores = jnp.dot(
@@ -163,10 +168,10 @@
             jnp.concatenate([host[k, chunk + n] for n in range(chunks)], axis=1),
             preferred_element_type=jnp.float32,
         )
-        after = row_rank[who, pl.ds(start, count), :]
+        before = row_rank[who, pl.ds(start, count), :]
         best = visit_best[who, pl.ds(start, count), :]
         for n in range(chunks):
-            before = lane_rank[k, pl.ds(chunk + n, 1), :]
+            after = lane_rank[k, pl.ds(chunk + n, 1), :]
             kept = jnp.where(before < after, scores[:, n * LANES : (n + 1) * LANES], LOW)
             best = jnp.maximum(best, kept)
             over = jnp.max(kept.reshape(count // 8, 8, LANES), axis=0)
@@ -193,7 +198,7 @@
             dst_ref=host_in.at[k, slot],
             send_sem=out_send.at[k * 4 + slot],
             recv_sem=out_recv.at[k * 4 + slot],
-            device_id=(b, part(y, slot)) if k == 0 else (low_b, part(low_y, slot)),
+            device_id=(b, part(y, slot)) if k == 0 else (next_b, part(next_y, slot)),
             device_id_type=MESH,
         )
 
@@ -203,7 +208,7 @@
             dst_ref=visit_in.at[who],
             send_sem=out_send.at[8 + who],
             recv_sem=out_recv.at[8 + who],
-            device_id=high if who == 1 else top,
+            device_id=behind if who == 1 else back,
             device_id_type=MESH,
         )
 
@@ -274,23 +279,23 @@
         one.wait_send()
     for one in results:
         one.wait_recv()
-    late = host_out[0, 0]
+    early = host_out[0, 0]
     for slot in range(1, 4):
-        late = jnp.maximum(late, host_in[0, slot])
-    late_ref[0] = late
-    late = host_in[1, 0]
+        early = jnp.maximum(early, host_in[0, slot])
+    early_ref[0] = early
+    early = host_in[1, 0]
     for slot in range(1, 4):
-        late = jnp.maximum(late, host_in[1, slot])
-    late_ref[1] = late
-    early_ref[0] = jnp.maximum(visit_out[0], visit_in[1])
-    early_ref[1] = visit_in[2]
+        early = jnp.maximum(early, host_in[1, slot])
+    early_ref[1] = early
+    late_ref[0] = jnp.maximum(visit_out[0], visit_in[1])
+    late_ref[1] = visit_in[2]
     for one in results:
         one.wait_send()
 
 
 def shards(blocks, embeddings, ranks):
     out = jax.ShapeDtypeStruct((2, 4, 128), jnp.float32)
-    late, early = pl.pallas_call(
+    early, late = pl.pallas_call(
         functools.partial(kernel, blocks),
         out_shape=(out, out),
         in_specs=[pl.BlockSpec(memory_space=pltpu.HBM)] * 2,
@@ -312,11 +317,12 @@
             pltpu.SemaphoreType.DMA((4,)),
             pltpu.SemaphoreType.DMA((9, PIECES)),
             pltpu.SemaphoreType.DMA((9, PIECES)),
+            pltpu.SemaphoreType.REGULAR,
             pltpu.SemaphoreType.DMA((11,)),
             pltpu.SemaphoreType.DMA((11,)),
         ],
         compiler_params=pltpu.CompilerParams(
-            collective_id=0, has_side_effects=True, vmem_limit_bytes=67043328 - (256 << 10)
+            collective_id=0, has_side_effects=True, vmem_limit_bytes=54976 << 10
         ),
     )(embeddings, ranks.reshape(-1, 128))
 
@@ -324,10 +330,9 @@
         return (jnp.maximum(one[0], other[0]), jnp.maximum(one[1], other[1]))
 
     start = jnp.float32(LOW)
-    late, early = lax.reduce(
-        (late.reshape(2, -1), early.reshape(2, -1)), (start, start), higher, (0,)
+    return lax.reduce(
+        (early.reshape(2, -1), late.reshape(2, -1)), (start, start), higher, (0,)
     )
-    return early, late
 
 
 def solution(mesh):

time: 58.5 us -> 55.2 us (0.944)
  the two profiles are of different devices: /device:TPU:32 before, /device:TPU:1 now
where the time goes in v4:
time: 55.2 us; the launch traced here: 55.1 us
  Pallas kernels  53.8 us (97%)
  between operations  0.64 us (1%)
  other arithmetic  0.61 us (1%)
    pallas_call x1, Pallas kernels, shards(): pl.pallas_call(functools.partial(kernel, blocks), out_shape=(out, out), i...  53.8 us

profile of v4, /device:TPU:1, one launch (start us, length us, event | category | flops | bytes accessed | tf_op | source)
XLA Modules:
  0.0 55.1 jit_solution(7321529760556119293)
XLA Ops:
  0.6 53.8 %shard_map.41 = (f32[2,4,128]{2,1,0:T(4,128)S(1)}, f32[2,4,128]{2,1,0:T(4,128)S(1)}) custom-call(f32[512,768]{1,0:T(8,128)} %emb_hbm.1, s32[1024,128]{1,0:T(8,128)} %bitcast.9), custom_call_target="tpu_custom_call" | custom-call | tf_op jit(solution)/shard_map/pallas_call | solution.py:298
  54.5 0.6 %bitcast_reduce_fusion = (f32[512]{0:T(512)}, f32[512]{0:T(512)}) fusion(f32[1,2,4,128]{3,2,1,0:T(4,128)S(1)} %bitcast.8, f32[1,2,4,128]{3,2,1,0:T(4,128)S(1)} %bitcast.7), kind=kLoop, calls=%fused_computation | loop fusion | flops 1024 | bytes 12288 | tf_op jit(solution)/shard_map/reduce | solution.py:333

commit v5 on v4

--- a/solution.py
+++ b/solution.py
@@ -10,11 +10,15 @@
 MESH = pl.DeviceIdType.MESH
 ROWS = 512
 WIDTH = 768
-PIECES = 8
-PIECE = ROWS // PIECES
+SIZES = (64, 192, 128, 128)
+ENDS = tuple(sum(SIZES[: i + 1]) for i in range(len(SIZES)))
+PIECES = len(SIZES)
+EARLY = max(1, sum(end <= 256 for end in ENDS))
+LOAD = 64
 LANES = 128
 CHUNKS = ROWS // LANES
-HALF = CHUNKS // 2
+TILES = ROWS // 128
+NEAR = 3
 LOW = -1.0
 
 VIS, VIS2, UP, FAR, SIDE, PAIR, PAIR_SIDE, PAIR_UP, PAIR_FAR = range(9)
@@ -62,7 +66,7 @@
         return ((base_y + slot // 2) % 2) * 2 + (c + slot % 2) % 2
 
     def rows(i):
-        return pl.ds(i * PIECE, PIECE)
+        return pl.ds(ENDS[i] - SIZES[i], SIZES[i])
 
     def copy(stream, i):
         if stream == VIS:
@@ -71,7 +75,7 @@
             src, dst, to = visit.at[1, rows(i)], visit.at[2, rows(i)], ahead
         elif stream == UP:
             src, dst, to = host.at[0, i], host.at[1, i], behind
-        elif stream == FAR and i < HALF:
+        elif stream == FAR and i < NEAR:
             src, dst, to = host.at[1, i], host.at[1, 2 * CHUNKS + i], side
         elif stream == FAR:
             src, dst, to = host.at[0, 2 * CHUNKS + i], host.at[1, 2 * CHUNKS + i], behind
@@ -101,8 +105,8 @@
         copy(stream, i).wait_recv()
 
     loads = [
-        pltpu.make_async_copy(emb_hbm.at[rows(i)], emb.at[rows(i)], load_sem.at[i])
-        for i in range(PIECES)
+        pltpu.make_async_copy(emb_hbm.at[at], emb.at[at], load_sem.at[i])
+        for i, at in enumerate(pl.ds(n, LOAD) for n in range(0, ROWS, LOAD))
     ]
     for load in loads:
         load.start()
@@ -129,18 +133,18 @@
 
     for j in range(CHUNKS):
         group = []
-        for i in (2 * j, 2 * j + 1):
-            loads[i].wait()
-            x = emb[rows(i), :]
+        for at in range(j * LANES, (j + 1) * LANES, LOAD):
+            loads[at // LOAD].wait()
+            x = emb[pl.ds(at, LOAD), :]
             squares = jnp.sum(x * x, axis=1, keepdims=True)
             unit = x * lax.rsqrt(squares + 1e-06)
-            visit[0, rows(i), :] = unit.astype(jnp.bfloat16)
+            visit[0, pl.ds(at, LOAD), :] = unit.astype(jnp.bfloat16)
             group.append(unit)
-            if i == 0:
+            if at == 0:
                 pl.semaphore_wait(barrier, 3)
                 pl.semaphore_signal(ready, inc=1, device_id=ahead, device_id_type=MESH)
-            else:
-                send(VIS, i - 1)
+            if at in ENDS:
+                send(VIS, ENDS.index(at))
         host[0, j] = jnp.concatenate(group, axis=0).T.astype(jnp.bfloat16)
         if j:
             first(j - 1)
@@ -170,20 +174,21 @@
         )
         before = row_rank[who, pl.ds(start, count), :]
         best = visit_best[who, pl.ds(start, count), :]
-        for n in range(chunks):
-            after = lane_rank[k, pl.ds(chunk + n, 1), :]
-            kept = jnp.where(before < after, scores[:, n * LANES : (n + 1) * LANES], LOW)
+        for n in range(chunks * LANES // 128):
+            at = chunk * LANES // 128 + n
+            after = lane_rank[k, pl.ds(at, 1), :]
+            kept = jnp.where(before < after, scores[:, n * 128 : (n + 1) * 128], LOW)
             best = jnp.maximum(best, kept)
-            over = jnp.max(kept.reshape(count // 8, 8, LANES), axis=0)
-            host_best[k, chunk + n] = jnp.maximum(host_best[k, chunk + n], over)
+            over = jnp.max(kept.reshape(count // 8, 8, 128), axis=0)
+            host_best[k, at] = jnp.maximum(host_best[k, at], over)
         visit_best[who, pl.ds(start, count), :] = best
 
     def half(k, which, who, start=0, count=ROWS):
         meet(k, which * 2 * CHUNKS, 2 * CHUNKS, who, start, count)
 
     def host_result(k):
-        for n in range(4 * CHUNKS):
-            host_out[k, n // CHUNKS, pl.ds(n % CHUNKS, 1), :] = jnp.max(
+        for n in range(4 * TILES):
+            host_out[k, n // TILES, pl.ds(n % TILES, 1), :] = jnp.max(
                 host_best[k, n], axis=0, keepdims=True
             )
 
@@ -222,16 +227,17 @@
         arrived(PAIR, j)
     half(0, 0, 0)
     for j in range(CHUNKS):
-        for i in (2 * j, 2 * j + 1):
-            arrived(VIS, i)
-            send(VIS2, i)
+        for i in range(PIECES):
+            if j * LANES < ENDS[i] <= (j + 1) * LANES:
+                arrived(VIS, i)
+                send(VIS2, i)
         arrived(SIDE, j)
         send(PAIR_SIDE, j)
-        if j >= HALF:
+        if j >= NEAR:
             send(FAR, j)
         arrived(UP, j)
         send(PAIR_UP, j)
-        if j < HALF:
+        if j < NEAR:
             send(FAR, j)
     half(0, 0, 1)
     for j in range(CHUNKS):
@@ -241,54 +247,57 @@
     for j in range(CHUNKS):
         arrived(PAIR_UP, j)
     half(1, 0, 1)
-    for j in range(HALF):
-        for n in (j, j + HALF):
-            arrived(FAR, n)
-            send(PAIR_FAR, n)
+    for j in (0, *range(NEAR, CHUNKS), *range(1, NEAR)):
+        arrived(FAR, j)
+        send(PAIR_FAR, j)
+        if j == 1:
+            for i in range(EARLY):
+                arrived(VIS2, i)
+            half(1, 0, 2, 0, ENDS[EARLY - 1])
     host_result(0)
     for t in range(4):
         visit_result(0, t)
     for slot in range(1, 4):
         give(host_copy(0, slot))
+    before_last = ENDS[PIECES - 2]
+    for i in range(EARLY, PIECES - 1):
+        arrived(VIS2, i)
+        half(1, 0, 2, ENDS[i - 1], SIZES[i])
     for j in range(CHUNKS):
         arrived(PAIR_FAR, j)
     half(1, 1, 1)
     for t in range(4):
         visit_result(1, t)
-    for i in range(PIECES // 2):
-        arrived(VIS2, i)
     give(visit_copy(1))
-    half(1, 0, 2, 0, ROWS // 2)
-    half(1, 1, 2, 0, ROWS // 2)
-    for i in (4, 5):
-        arrived(VIS2, i)
-    half(1, 0, 2, 4 * PIECE, 2 * PIECE)
-    half(1, 1, 2, 4 * PIECE, 2 * PIECE)
-    for t in range(3):
+    half(1, 1, 2, 0, before_last)
+    for t in range(before_last // 128):
         visit_result(2, t)
-    for i in (6, 7):
-        arrived(VIS2, i)
-        meet(1, 0, 4 * CHUNKS, 2, i * PIECE, PIECE)
+    arrived(VIS2, PIECES - 1)
+    half(1, 0, 2, before_last, ROWS - before_last)
+    half(1, 1, 2, before_last, ROWS - before_last)
     host_result(1)
-    visit_result(2, 3)
     for slot in range(4):
         give(host_copy(1, slot))
+    for t in range(before_last // 128, 4):
+        visit_result(2, t)
     give(visit_copy(2))
 
     for one in started:
         one.wait_send()
-    for one in results:
+    for one in results[:4]:
         one.wait_recv()
     early = host_out[0, 0]
     for slot in range(1, 4):
         early = jnp.maximum(early, host_in[0, slot])
     early_ref[0] = early
+    late_ref[0] = jnp.maximum(visit_out[0], visit_in[1])
+    for one in results[4:]:
+        one.wait_recv()
+    late_ref[1] = visit_in[2]
     early = host_in[1, 0]
     for slot in range(1, 4):
         early = jnp.maximum(early, host_in[1, slot])
     early_ref[1] = early
-    late_ref[0] = jnp.maximum(visit_out[0], visit_in[1])
-    late_ref[1] = visit_in[2]
     for one in results:
         one.wait_send()
 
@@ -307,16 +316,16 @@
             pltpu.VMEM((3, ROWS, WIDTH), jnp.bfloat16),
             pltpu.VMEM((2, 16, 128), jnp.float32),
             pltpu.VMEM((3, ROWS, 128), jnp.float32),
-            pltpu.VMEM((2, 4 * CHUNKS, 8, LANES), jnp.float32),
+            pltpu.VMEM((2, 4 * TILES, 8, 128), jnp.float32),
             pltpu.VMEM((3, ROWS, 128), jnp.float32),
             pltpu.VMEM((2, 4, 4, 128), jnp.float32),
             pltpu.VMEM((2, 4, 4, 128), jnp.float32),
             pltpu.VMEM((3, 4, 128), jnp.float32),
             pltpu.VMEM((3, 4, 128), jnp.float32),
-            pltpu.SemaphoreType.DMA((PIECES,)),
+            pltpu.SemaphoreType.DMA((ROWS // LOAD,)),
             pltpu.SemaphoreType.DMA((4,)),
-            pltpu.SemaphoreType.DMA((9, PIECES)),
-            pltpu.SemaphoreType.DMA((9, PIECES)),
+            pltpu.SemaphoreType.DMA((9, max(PIECES, CHUNKS))),
+            pltpu.SemaphoreType.DMA((9, max(PIECES, CHUNKS))),
             pltpu.SemaphoreType.REGULAR,
             pltpu.SemaphoreType.DMA((11,)),
             pltpu.SemaphoreType.DMA((11,)),

time: 55.2 us -> 53 us (0.960)
  Pallas kernels: 53.8 us -> 51.7 us
    pallas_call x1, Pallas kernels: 53.8 us -> 51.7 us  [shards(): pl.pallas_call(functools.partial(kernel, blocks), out_shape=(out, out), i...]
where the time goes in v5:
time: 53 us; the launch traced here: 52.9 us
  Pallas kernels  51.7 us (98%)
  between operations  0.64 us (1%)
  other arithmetic  0.61 us (1%)
    pallas_call x1, Pallas kernels, shards(): pl.pallas_call(functools.partial(kernel, blocks), out_shape=(out, out), i...  51.7 us

profile of v5, /device:TPU:1, one launch (start us, length us, event | category | flops | bytes accessed | tf_op | source)
XLA Modules:
  0.0 52.9 jit_solution(12419482326940513123)
XLA Ops:
  0.6 51.7 %shard_map.41 = (f32[2,4,128]{2,1,0:T(4,128)S(1)}, f32[2,4,128]{2,1,0:T(4,128)S(1)}) custom-call(f32[512,768]{1,0:T(8,128)} %emb_hbm.1, s32[1024,128]{1,0:T(8,128)} %bitcast.9), custom_call_target="tpu_custom_call" | custom-call | tf_op jit(solution)/shard_map/pallas_call | solution.py:307
  52.3 0.6 %bitcast_reduce_fusion = (f32[512]{0:T(512)}, f32[512]{0:T(512)}) fusion(f32[1,2,4,128]{3,2,1,0:T(4,128)S(1)} %bitcast.8, f32[1,2,4,128]{3,2,1,0:T(4,128)S(1)} %bitcast.7), kind=kLoop, calls=%fused_computation | loop fusion | flops 1024 | bytes 12288 | tf_op jit(solution)/shard_map/reduce | solution.py:342

commit v6 on v5

--- a/solution.py
+++ b/solution.py
@@ -186,10 +186,10 @@
     def half(k, which, who, start=0, count=ROWS):
         meet(k, which * 2 * CHUNKS, 2 * CHUNKS, who, start, count)
 
-    def host_result(k):
-        for n in range(4 * TILES):
-            host_out[k, n // TILES, pl.ds(n % TILES, 1), :] = jnp.max(
-                host_best[k, n], axis=0, keepdims=True
+    def host_result(k, slot):
+        for n in range(TILES):
+            host_out[k, slot, pl.ds(n, 1), :] = jnp.max(
+                host_best[k, slot * TILES + n], axis=0, keepdims=True
             )
 
     def visit_result(who, t):
@@ -254,7 +254,8 @@
             for i in range(EARLY):
                 arrived(VIS2, i)
             half(1, 0, 2, 0, ENDS[EARLY - 1])
-    host_result(0)
+    for slot in range(4):
+        host_result(0, slot)
     for t in range(4):
         visit_result(0, t)
     for slot in range(1, 4):
@@ -273,11 +274,12 @@
     for t in range(before_last // 128):
         visit_result(2, t)
     arrived(VIS2, PIECES - 1)
-    half(1, 0, 2, before_last, ROWS - before_last)
-    half(1, 1, 2, before_last, ROWS - before_last)
-    host_result(1)
-    for slot in range(4):
-        give(host_copy(1, slot))
+    for which in (1, 0):
+        half(1, which, 2, before_last, ROWS - before_last)
+        for slot in (2 * which, 2 * which + 1):
+            host_result(1, slot)
+        for slot in (2 * which, 2 * which + 1):
+            give(host_copy(1, slot))
     for t in range(before_last // 128, 4):
         visit_result(2, t)
     give(visit_copy(2))

time: 53 us -> 52.9 us (level)
  no operation moved by 1% of the time
where the time goes in v6:
time: 52.9 us; the launch traced here: 52.8 us
  Pallas kernels  51.6 us (98%)
  between operations  0.64 us (1%)
  other arithmetic  0.61 us (1%)
    pallas_call x1, Pallas kernels, shards(): pl.pallas_call(functools.partial(kernel, blocks), out_shape=(out, out), i...  51.6 us

profile of v6, /device:TPU:1, one launch (start us, length us, event | category | flops | bytes accessed | tf_op | source)
XLA Modules:
  0.0 52.8 jit_solution(1203164455230351007)
XLA Ops:
  0.6 51.6 %shard_map.41 = (f32[2,4,128]{2,1,0:T(4,128)S(1)}, f32[2,4,128]{2,1,0:T(4,128)S(1)}) custom-call(f32[512,768]{1,0:T(8,128)} %emb_hbm.1, s32[1024,128]{1,0:T(8,128)} %bitcast.9), custom_call_target="tpu_custom_call" | custom-call | tf_op jit(solution)/shard_map/pallas_call | solution.py:309
  52.2 0.6 %bitcast_reduce_fusion = (f32[512]{0:T(512)}, f32[512]{0:T(512)}) fusion(f32[1,2,4,128]{3,2,1,0:T(4,128)S(1)} %bitcast.8, f32[1,2,4,128]{3,2,1,0:T(4,128)S(1)} %bitcast.7), kind=kLoop, calls=%fused_computation | loop fusion | flops 1024 | bytes 12288 | tf_op jit(solution)/shard_map/reduce | solution.py:344

commit v7 on v6

--- a/solution.py
+++ b/solution.py
@@ -47,6 +47,8 @@
     send_sem,
     recv_sem,
     ready,
+    relay,
+    relay_sem,
     out_send,
     out_recv,
 ):
@@ -61,6 +63,9 @@
     back = (back_b, back_y * 2 + c)
     side = (b, (1 - y) * 2 + c)
     pair = (b, y * 2 + 1 - c)
+    place = b % 16
+    over = ((b + blocks - 8) % blocks, (1 - y) * 2 + c)
+    under = ((b + 8) % blocks, (1 - y) * 2 + c)
 
     def part(base_y, slot):
         return ((base_y + slot // 2) % 2) * 2 + (c + slot % 2) % 2
@@ -94,6 +99,22 @@
             device_id_type=MESH,
         )
 
+    def detour(src, dst, sent, got, to):
+        return pltpu.make_async_remote_copy(
+            src_ref=src,
+            dst_ref=dst,
+            send_sem=sent,
+            recv_sem=got,
+            device_id=to,
+            device_id_type=MESH,
+        )
+
+    leave = detour(visit.at[1, rows(0)], relay, send_sem.at[VIS2, 0], relay_sem.at[1], over)
+    along = detour(relay, relay, relay_sem.at[0], relay_sem.at[1], ahead)
+    back_in = detour(
+        relay, visit.at[2, rows(0)], relay_sem.at[0], recv_sem.at[VIS2, 0], under
+    )
+
     started = []
 
     def send(stream, i):
@@ -126,6 +147,20 @@
 
     host_best[...] = jnp.full_like(host_best, LOW)
     visit_best[...] = jnp.full_like(visit_best, LOW)
+
+
+    @pl.when(place == 6)
+    def _():
+        pl.semaphore_signal(barrier, inc=1, device_id=under, device_id_type=MESH)
+
+    @pl.when(place == 15)
+    def _():
+        pl.semaphore_signal(barrier, inc=1, device_id=over, device_id_type=MESH)
+
+    is_seventh = (place // 14) * (1 - place // 15)
+    is_relay = (b % 8 // 7) * (1 - place // 8)
+    pl.semaphore_wait(barrier, 3 + is_seventh + is_relay)
+    pl.semaphore_signal(ready, inc=1, device_id=ahead, device_id_type=MESH)
 
     def first(j):
         for stream in (SIDE, PAIR):
@@ -140,9 +175,6 @@
             unit = x * lax.rsqrt(squares + 1e-06)
             visit[0, pl.ds(at, LOAD), :] = unit.astype(jnp.bfloat16)
             group.append(unit)
-            if at == 0:
-                pl.semaphore_wait(barrier, 3)
-                pl.semaphore_signal(ready, inc=1, device_id=ahead, device_id_type=MESH)
             if at in ENDS:
                 send(VIS, ENDS.index(at))
         host[0, j] = jnp.concatenate(group, axis=0).T.astype(jnp.bfloat16)
@@ -166,25 +198,26 @@
     for j in range(CHUNKS):
         send(UP, j)
 
-    def meet(k, chunk, chunks, who, start, count):
+    def meet(k, chunks, who, start=0, count=ROWS):
         scores = jnp.dot(
             visit[who, pl.ds(start, count), :],
-            jnp.concatenate([host[k, chunk + n] for n in range(chunks)], axis=1),
+            jnp.concatenate([host[k, n] for n in chunks], axis=1),
             preferred_element_type=jnp.float32,
         )
         before = row_rank[who, pl.ds(start, count), :]
         best = visit_best[who, pl.ds(start, count), :]
-        for n in range(chunks * LANES // 128):
-            at = chunk * LANES // 128 + n
-            after = lane_rank[k, pl.ds(at, 1), :]
-            kept = jnp.where(before < after, scores[:, n * 128 : (n + 1) * 128], LOW)
+        for at, n in enumerate(chunks):
+            after = lane_rank[k, pl.ds(n, 1), :]
+            kept = jnp.where(before < after, scores[:, at * LANES : (at + 1) * LANES], LOW)
             best = jnp.maximum(best, kept)
-            over = jnp.max(kept.reshape(count // 8, 8, 128), axis=0)
-            host_best[k, at] = jnp.maximum(host_best[k, at], over)
+            over = jnp.max(kept.reshape(count // 8, 8, LANES), axis=0)
+            host_best[k, n] = jnp.maximum(host_best[k, n], over)
         visit_best[who, pl.ds(start, count), :] = best
 
-    def half(k, which, who, start=0, count=ROWS):
-        meet(k, which * 2 * CHUNKS, 2 * CHUNKS, who, start, count)
+    near = range(2 * CHUNKS)
+    far = range(2 * CHUNKS, 4 * CHUNKS)
+    lots = ((0, *range(NEAR, CHUNKS)), range(1, NEAR))
+    far_lots = [[2 * CHUNKS + j + n for n in (0, CHUNKS) for j in lot] for lot in lots]
 
     def host_result(k, slot):
         for n in range(TILES):
@@ -225,76 +258,109 @@
 
     for j in range(CHUNKS):
         arrived(PAIR, j)
-    half(0, 0, 0)
+    meet(0, near, 0)
     for j in range(CHUNKS):
         for i in range(PIECES):
             if j * LANES < ENDS[i] <= (j + 1) * LANES:
                 arrived(VIS, i)
-                send(VIS2, i)
+                if i:
+                    send(VIS2, i)
+                    continue
+                started.append(copy(VIS2, 0))
+
+                @pl.when(place != 14)
+                def _():
+                    copy(VIS2, 0).start()
+
+                @pl.when(place == 14)
+                def _():
+                    leave.start()
         arrived(SIDE, j)
         send(PAIR_SIDE, j)
         if j >= NEAR:
             send(FAR, j)
+        if j == CHUNKS - 1:
+            meet(0, near, 1)
+            for n in range(CHUNKS):
+                arrived(PAIR_SIDE, n)
+            meet(0, far, 0)
+            meet(0, far, 1)
         arrived(UP, j)
         send(PAIR_UP, j)
         if j < NEAR:
             send(FAR, j)
-    half(0, 0, 1)
-    for j in range(CHUNKS):
-        arrived(PAIR_SIDE, j)
-    half(0, 1, 0)
-    half(0, 1, 1)
+        if j == 0:
+
+            @pl.when(place == 6)
+            def _():
+                along.wait_recv()
+                along.start()
     for j in range(CHUNKS):
         arrived(PAIR_UP, j)
-    half(1, 0, 1)
-    for j in (0, *range(NEAR, CHUNKS), *range(1, NEAR)):
-        arrived(FAR, j)
-        send(PAIR_FAR, j)
-        if j == 1:
-            for i in range(EARLY):
-                arrived(VIS2, i)
-            half(1, 0, 2, 0, ENDS[EARLY - 1])
+    meet(1, near, 1)
     for slot in range(4):
         host_result(0, slot)
     for t in range(4):
         visit_result(0, t)
     for slot in range(1, 4):
         give(host_copy(0, slot))
-    before_last = ENDS[PIECES - 2]
+
+    @pl.when(place == 7)
+    def _():
+        along.wait_recv()
+        back_in.start()
+
+    for j in lots[0]:
+        arrived(FAR, j)
+        send(PAIR_FAR, j)
+    for j in lots[0]:
+        arrived(PAIR_FAR, j)
+    meet(1, far_lots[0], 1)
+    for n, j in enumerate(lots[1]):
+        arrived(FAR, j)
+        send(PAIR_FAR, j)
+        if n == 0:
+            for i in range(EARLY):
+                arrived(VIS2, i)
+            meet(1, near, 2, 0, ENDS[EARLY - 1])
+            meet(1, far_lots[0], 2, 0, ENDS[EARLY - 1])
     for i in range(EARLY, PIECES - 1):
         arrived(VIS2, i)
-        half(1, 0, 2, ENDS[i - 1], SIZES[i])
-    for j in range(CHUNKS):
+        meet(1, near, 2, ENDS[i - 1], SIZES[i])
+        meet(1, far_lots[0], 2, ENDS[i - 1], SIZES[i])
+    before_last = ENDS[PIECES - 2]
+    for j in lots[1]:
         arrived(PAIR_FAR, j)
-    half(1, 1, 1)
-    for t in range(4):
-        visit_result(1, t)
-    give(visit_copy(1))
-    half(1, 1, 2, 0, before_last)
-    for t in range(before_last // 128):
-        visit_result(2, t)
+    meet(1, far_lots[1], 1)
+    meet(1, far_lots[1], 2, 0, before_last)
     arrived(VIS2, PIECES - 1)
-    for which in (1, 0):
-        half(1, which, 2, before_last, ROWS - before_last)
+    for which, chunks in ((1, far), (0, near)):
+        meet(1, chunks, 2, before_last, ROWS - before_last)
         for slot in (2 * which, 2 * which + 1):
             host_result(1, slot)
         for slot in (2 * which, 2 * which + 1):
             give(host_copy(1, slot))
-    for t in range(before_last // 128, 4):
-        visit_result(2, t)
-    give(visit_copy(2))
+    for who in (2, 1):
+        for t in range(4):
+            visit_result(who, t)
+        give(visit_copy(who))
 
     for one in started:
         one.wait_send()
-    for one in results[:4]:
+
+    @pl.when((place == 6) | (place == 7))
+    def _():
+        along.wait_send()
+
+    for one in results[:3]:
         one.wait_recv()
     early = host_out[0, 0]
     for slot in range(1, 4):
         early = jnp.maximum(early, host_in[0, slot])
     early_ref[0] = early
+    for one in results[3:]:
+        one.wait_recv()
     late_ref[0] = jnp.maximum(visit_out[0], visit_in[1])
-    for one in results[4:]:
-        one.wait_recv()
     late_ref[1] = visit_in[2]
     early = host_in[1, 0]
     for slot in range(1, 4):
@@ -329,6 +395,8 @@
             pltpu.SemaphoreType.DMA((9, max(PIECES, CHUNKS))),
             pltpu.SemaphoreType.DMA((9, max(PIECES, CHUNKS))),
             pltpu.SemaphoreType.REGULAR,
+            pltpu.VMEM((SIZES[0], WIDTH), jnp.bfloat16),
+            pltpu.SemaphoreType.DMA((2,)),
             pltpu.SemaphoreType.DMA((11,)),
             pltpu.SemaphoreType.DMA((11,)),
         ],

time: 52.9 us -> 51.8 us (0.979)
  Pallas kernels: 51.6 us -> 50.5 us
    pallas_call x1, Pallas kernels: 51.6 us -> 50.5 us  [shards(): pl.pallas_call(functools.partial(kernel, blocks), out_shape=(out, out), i...]
where the time goes in v7:
time: 51.8 us; the launch traced here: 51.7 us
  Pallas kernels  50.5 us (97%)
  between operations  0.64 us (1%)
  other arithmetic  0.61 us (1%)
    pallas_call x1, Pallas kernels, shards(): pl.pallas_call(functools.partial(kernel, blocks), out_shape=(out, out), i...  50.5 us

profile of v7, /device:TPU:1, one launch (start us, length us, event | category | flops | bytes accessed | tf_op | source)
XLA Modules:
  0.0 51.7 jit_solution(16208920614111782202)
XLA Ops:
  0.6 50.5 %shard_map.41 = (f32[2,4,128]{2,1,0:T(4,128)S(1)}, f32[2,4,128]{2,1,0:T(4,128)S(1)}) custom-call(f32[512,768]{1,0:T(8,128)} %emb_hbm.1, s32[1024,128]{1,0:T(8,128)} %bitcast.9), custom_call_target="tpu_custom_call" | custom-call | tf_op jit(solution)/shard_map/pallas_call | solution.py:375
  51.1 0.6 %bitcast_reduce_fusion = (f32[512]{0:T(512)}, f32[512]{0:T(512)}) fusion(f32[1,2,4,128]{3,2,1,0:T(4,128)S(1)} %bitcast.8, f32[1,2,4,128]{3,2,1,0:T(4,128)S(1)} %bitcast.7), kind=kLoop, calls=%fused_computation | loop fusion | flops 1024 | bytes 12288 | tf_op jit(solution)/shard_map/reduce | solution.py:412

commit v8 on v7

--- a/solution.py
+++ b/solution.py
@@ -334,7 +334,7 @@
     meet(1, far_lots[1], 1)
     meet(1, far_lots[1], 2, 0, before_last)
     arrived(VIS2, PIECES - 1)
-    for which, chunks in ((1, far), (0, near)):
+    for which, chunks in ((0, near), (1, far)):
         meet(1, chunks, 2, before_last, ROWS - before_last)
         for slot in (2 * which, 2 * which + 1):
             host_result(1, slot)

time: 51.8 us -> 51.4 us (level)
  no operation moved by 1% of the time
where the time goes in v8:
time: 51.4 us; the launch traced here: 51.3 us
  Pallas kernels  50.1 us (97%)
  between operations  0.64 us (1%)
  other arithmetic  0.61 us (1%)
    pallas_call x1, Pallas kernels, shards(): pl.pallas_call(functools.partial(kernel, blocks), out_shape=(out, out), i...  50.1 us

profile of v8, /device:TPU:1, one launch (start us, length us, event | category | flops | bytes accessed | tf_op | source)
XLA Modules:
  0.0 51.3 jit_solution(7645178325508220715)
XLA Ops:
  0.6 50.1 %shard_map.41 = (f32[2,4,128]{2,1,0:T(4,128)S(1)}, f32[2,4,128]{2,1,0:T(4,128)S(1)}) custom-call(f32[512,768]{1,0:T(8,128)} %emb_hbm.1, s32[1024,128]{1,0:T(8,128)} %bitcast.9), custom_call_target="tpu_custom_call" | custom-call | tf_op jit(solution)/shard_map/pallas_call | solution.py:375
  50.7 0.6 %bitcast_reduce_fusion = (f32[512]{0:T(512)}, f32[512]{0:T(512)}) fusion(f32[1,2,4,128]{3,2,1,0:T(4,128)S(1)} %bitcast.8, f32[1,2,4,128]{3,2,1,0:T(4,128)S(1)} %bitcast.7), kind=kLoop, calls=%fused_computation | loop fusion | flops 1024 | bytes 12288 | tf_op jit(solution)/shard_map/reduce | solution.py:412

commit v9 on v8

--- a/solution.py
+++ b/solution.py
@@ -184,6 +184,10 @@
     for load in rank_loads:
         load.wait()
     first(CHUNKS - 1)
+    pl.semaphore_wait(ready, 1)
+    for j in range(CHUNKS):
+        send(UP, j)
+
     for k, base_y in ((0, y), (1, next_y)):
         for slot in range(4):
             lane_rank[k, pl.ds(slot * 4, 4), :] = raw[
@@ -193,10 +197,6 @@
         for t in range(4):
             line = raw[at, pl.ds(part(base_y, 0) * 4 + t, 1), :].astype(jnp.float32)
             row_rank[k, pl.ds(t * 128, 128), :] = jnp.broadcast_to(line, (128, 128)).T
-
-    pl.semaphore_wait(ready, 1)
-    for j in range(CHUNKS):
-        send(UP, j)
 
     def meet(k, chunks, who, start=0, count=ROWS):
         scores = jnp.dot(

time: 51.4 us -> 51.4 us (level)
  no operation moved by 1% of the time
where the time goes in v9:
time: 51.4 us; the launch traced here: 51.3 us
  Pallas kernels  50.1 us (97%)
  between operations  0.64 us (1%)
  other arithmetic  0.61 us (1%)
    pallas_call x1, Pallas kernels, shards(): pl.pallas_call(functools.partial(kernel, blocks), out_shape=(out, out), i...  50.1 us

profile of v9, /device:TPU:1, one launch (start us, length us, event | category | flops | bytes accessed | tf_op | source)
XLA Modules:
  0.0 51.3 jit_solution(1587761638839542042)
XLA Ops:
  0.6 50.1 %shard_map.41 = (f32[2,4,128]{2,1,0:T(4,128)S(1)}, f32[2,4,128]{2,1,0:T(4,128)S(1)}) custom-call(f32[512,768]{1,0:T(8,128)} %emb_hbm.1, s32[1024,128]{1,0:T(8,128)} %bitcast.9), custom_call_target="tpu_custom_call" | custom-call | tf_op jit(solution)/shard_map/pallas_call | solution.py:375
  50.7 0.6 %bitcast_reduce_fusion = (f32[512]{0:T(512)}, f32[512]{0:T(512)}) fusion(f32[1,2,4,128]{3,2,1,0:T(4,128)S(1)} %bitcast.8, f32[1,2,4,128]{3,2,1,0:T(4,128)S(1)} %bitcast.7), kind=kLoop, calls=%fused_computation | loop fusion | flops 1024 | bytes 12288 | tf_op jit(solution)/shard_map/reduce | solution.py:412
